TPU v7x, 32 devices: a whole 2x2x4 slice. The times are simulated.
32 devices in a mesh: pix: 32 (over z, y, x, core).
Axes of the slice: x: 2, y: 2, z: 4, core: 2. Of those that a mesh axis runs over, the one named last changes fastest.
Arguments:
- green: float32 [2048, 6144], P('pix'), may hold values from -200 to 200, as said below
- sketch: float32 [6144, 128], P('pix'), may hold values from -0.078125 to 0.078125
Outputs:
- basis: float32 [2048, 128], P('pix')
- projection: float32 [6144, 128], P('pix')
- spectrum_gram: float32 [128, 128], replicated
Inputs may be any that keep to these rules, and one draw needn't show every extreme that they name: `green`: finite real entries; each patch's column has its own scale.
All inputs are finite; a program needn't handle non-finite values.
Results may differ from a plain program's by a relative error of at most 0.000086.
Values sent between devices are 32-bit elements; how exact they have to be, the bound alone decides.
No kernel may reach another device: no remote copies, remote signals or barrier semaphores. Data moves between devices by JAX's collectives and lax.ppermute only.
A program may use at most 64 MiB of HBM per device.

v0:
```python
import jax
import jax.numpy as jnp
from jax import lax
from jax.sharding import PartitionSpec as P

PATCHES = 6144


def body(green, sketch):
    highest = lax.Precision.HIGHEST
    rows_here = green.shape[0]
    devices_pix = lax.axis_size("pix")
    total_pixels = rows_here * devices_pix
    columns = green
    sketched = jnp.dot(
        columns,
        lax.all_gather(sketch, "pix", axis=0, tiled=True),
        precision=highest,
        preferred_element_type=jnp.float32,
    )
    local_gram = jnp.dot(
        sketched.T, sketched, precision=highest, preferred_element_type=jnp.float32
    )
    columns = green
    raw_proj = lax.psum_scatter(
        lax.dot_general(
            columns,
            sketched,
            (((0,), (0,)), ((), ())),
            precision=highest,
            preferred_element_type=jnp.float32,
        ),
        "pix",
        scatter_dimension=0,
        tiled=True,
    )
    gram = lax.psum(local_gram, "pix")
    lower = jnp.linalg.cholesky(gram)
    orthonormal = jax.scipy.linalg.solve_triangular(lower, sketched.T, lower=True).T
    projection = jax.scipy.linalg.solve_triangular(lower, raw_proj.T, lower=True).T
    basis = jnp.sqrt(jnp.float32(total_pixels)) * orthonormal
    local_spec = jnp.dot(
        projection.T, projection, precision=highest, preferred_element_type=jnp.float32
    )
    spectrum_gram = lax.psum(local_spec, "pix") / jnp.float32(PATCHES)
    return (basis, projection, spectrum_gram)


def solution(mesh):
    in_specs = (P("pix", None), P("pix", None))
    out_specs = (P("pix", None), P("pix", None), P())
    return jax.shard_map(body, mesh=mesh, in_specs=in_specs, out_specs=out_specs, check_vma=False)
```

profile of v0, /device:TPU:1, one launch (start us, length us, event | category | flops | bytes accessed | tf_op | source)
XLA Modules:
  0.0 439.5 jit_solution(5103394524616839399)
XLA Ops:
  7.2 0.0 all-gather.2.cloned.1.call-start
  7.2 0.7 all-gather.2.cloned.1.call-update
  7.9 0.0 all-reduce.3.cloned.1.call-start
  8.0 64.5 %all-gather.2.cloned.1.call-done = f32[6144,128]{1,0:T(8,128)} async-done(((f32[192,128]{1,0:T(8,128)}), f32[6144,128]{1,0:T(8,128)}) %all-gather.2.cloned.1.call-update) | async-done | bytes 3145744 | tf_op jit(solution)/shard_map/all_gather | solution.py:17
  72.4 3.9 fusion.5
  76.3 0.9 fusion.6
  77.3 0.0 reduce-scatter.4.cloned.1.call-start
  77.3 4.4 convolution_bitcast_fusion
  81.7 3.6 copy.10
  85.2 0.0 reduce-scatter.4.cloned.1.call-update
  85.3 0.2 all-reduce.5.cloned.1.call-start
  85.5 112.7 %all-reduce.3.cloned.1.call-done = f32[128,128]{0,1:T(8,128)} async-done(((f32[128,128]{0,1:T(8,128)}), f32[128,128]{0,1:T(8,128)}) %all-reduce.3.cloned.1.call-update) | async-done | bytes 65552 | tf_op jit(solution)/shard_map/psum | solution.py:37
  198.2 0.9 copy.8
  199.1 0.9 fusion.4
  200.0 11.7 %cholesky.16 = f32[128,128]{1,0:T(8,128)S(1)} custom-call(f32[128,128]{1,0:T(8,128)S(1)} %fusion.4), custom_call_target="Cholesky" | custom-call | tf_op jit(solution)/shard_map/jit(cholesky)/cholesky | solution.py:38
  211.7 0.6 compare_reduce_fusion
  212.4 0.7 fusion
  213.0 9.8 %custom-call.10 = f32[1,128,128]{1,2,0:T(8,128)S(1)} custom-call(f32[1,128,128]{2,1,0:T(8,128)S(1)} %fusion), custom_call_target="InvertDiagBlocksLowerTriangular" | custom-call | tf_op jit(solution)/shard_map/jit(_solve_triangular)/triangular_solve | solution.py:39
  222.9 80.8 %reduce-scatter.4.cloned.1.call-done = f32[192,128]{1,0:T(8,128)} async-done(((f32[6144,128]{1,0:T(8,128)}), f32[192,128]{1,0:T(8,128)}) %reduce-scatter.4.cloned.1.call-update) | async-done | bytes 98320
  303.6 1.1 fusion.1
  304.8 1.1 fusion.7
  305.9 0.8 convolution_multiply_fusion
  306.7 124.8 %all-reduce.5.cloned.1.call-done = f32[128,128]{1,0:T(8,128)} async-done(((f32[128,128]{1,0:T(8,128)}), f32[128,128]{1,0:T(8,128)}) %all-reduce.5.cloned.1.call-update) | async-done | bytes 65552 | tf_op jit(solution)/shard_map/psum | solution.py:45
  431.5 1.5 broadcast_multiply_fusion
  (7 shorter events, 0.1 us)
Async XLA Ops:
  7.2 65.3 %copy-start = (f32[64,6144]{1,0:T(8,128)S(1)}, f32[64,6144]{1,0:T(8,128)}, u32[]{:S(2)}) copy-start(f32[64,6144]{1,0:T(8,128)} %param.2) | copy-start | bytes 4718596
  7.2 65.2 %all-gather.2.cloned.1.call-start = ((), (), s32[]{:S(2)}) async-start(), calls=%async_computation.1 | async-start | bytes 3244032 | tf_op jit(solution)/shard_map/all_gather | solution.py:17
  7.9 190.3 %all-reduce.3.cloned.1.call-start = ((), (), s32[]{:S(2)}) async-start(), calls=%async_computation.2 | async-start | bytes 131072 | tf_op jit(solution)/shard_map/psum | solution.py:37
  77.3 226.4 %reduce-scatter.4.cloned.1.call-start = ((), (), s32[]{:S(2)}) async-start(), calls=%async_computation.4 | async-start | bytes 3244032
  85.3 346.3 %all-reduce.5.cloned.1.call-start = ((), (), s32[]{:S(2)}) async-start(), calls=%async_computation.3 | async-start | bytes 131072 | tf_op jit(solution)/shard_map/psum | solution.py:45
  304.8 128.2 %copy-start.1 = (f32[128,192]{0,1:T(8,128)}, f32[128,192]{0,1:T(8,128)S(1)}, u32[]{:S(2)}) copy-start(f32[128,192]{0,1:T(8,128)S(1)} %fusion.1) | copy-start | bytes 294916
Sparse Core Ops, SparseCore 0:
  10.9 61.5 all-gather.1
  78.6 119.5 all-reduce.2
  203.6 99.9 reduce-scatter.3
  309.6 121.8 all-reduce.4
where the time goes:
time: 440 us
  waiting for transfers between devices  384 us (87%)
  other arithmetic  25.2 us (6%)
  between operations  13.8 us (3%)
  matrix products  12.2 us (3%)
  local copies, waits for them, and re-layouts  4.5 us (1%)
    psum x1, waiting for transfers between devices, body(): spectrum_gram = lax.psum(local_spec, 'pix') / jnp.float32(PATCHES)  125 us
    psum x1, waiting for transfers between devices, body(): gram = lax.psum(local_gram, 'pix')  113 us
    unnamed x5, waiting for transfers between devices  81.5 us
    all_gather x1, waiting for transfers between devices, body(): lax.all_gather(sketch, 'pix', axis=0, tiled=True)  64.5 us
    another operation x3, other arithmetic, body(): lower = jnp.linalg.cholesky(gram)  12.4 us
    another operation x2, other arithmetic, body(): jax.scipy.linalg.solve_triangular(lower, sketched.T, lower=True)  10.5 us
  transfers between devices with their start and end apart: 4, of which 4 were waited for; matrix products, arithmetic and copies ran while one was open for 8% of the time, Pallas kernels for 0%

commit v1 on v0

--- a/solution.py
+++ b/solution.py
@@ -42,7 +42,7 @@
     local_spec = jnp.dot(
         projection.T, projection, precision=highest, preferred_element_type=jnp.float32
     )
-    spectrum_gram = lax.psum(local_spec, "pix") / jnp.float32(PATCHES)
+    spectrum_gram = jnp.sum(lax.all_gather(local_spec, "pix"), axis=0) / jnp.float32(PATCHES)
     return (basis, projection, spectrum_gram)
 
 

time: 440 us -> 374 us (0.85)
  waiting for transfers between devices: 384 us -> 316 us
    psum x1 -> x0, waiting for transfers between devices: 125 us -> none  [body(): spectrum_gram = lax.psum(local_spec, 'pix') / jnp.float32(PATCHES)]
    all_gather x0 -> x1, waiting for transfers between devices: none -> 57.6 us  [body(): lax.all_gather(local_spec, 'pix')]
  transfers between devices with their start and end apart: 4 -> 4, of which waited for: 4 -> 4; matrix products, arithmetic and copies ran while one was open for 8% -> 9% of each run, Pallas kernels for 0% -> 0%
where the time goes in v1:
time: 374 us; the launch traced here: 373 us
  waiting for transfers between devices  316 us (84%)
  other arithmetic  26.1 us (7%)
  between operations  13.8 us (4%)
  matrix products  12.2 us (3%)
  local copies, waits for them, and re-layouts  4.5 us (1%)
    psum x1, waiting for transfers between devices, body(): gram = lax.psum(local_gram, 'pix')  113 us
    unnamed x5, waiting for transfers between devices  81.5 us
    all_gather x1, waiting for transfers between devices, body(): lax.all_gather(sketch, 'pix', axis=0, tiled=True)  64.5 us
    all_gather x1, waiting for transfers between devices, body(): lax.all_gather(local_spec, 'pix')  57.6 us
    another operation x3, other arithmetic, body(): lower = jnp.linalg.cholesky(gram)  12.4 us
    another operation x2, other arithmetic, body(): jax.scipy.linalg.solve_triangular(lower, sketched.T, lower=True)  10.5 us
  transfers between devices with their start and end apart: 4, of which 4 were waited for; matrix products, arithmetic and copies ran while one was open for 9% of the time, Pallas kernels for 0%

profile of v1, /device:TPU:1, one launch (start us, length us, event | category | flops | bytes accessed | tf_op | source)
XLA Modules:
  0.0 373.1 jit_solution(11456021701532989510)
XLA Ops:
  7.2 0.0 all-gather.4.cloned.1.call-start
  7.2 0.7 all-gather.4.cloned.1.call-update
  7.9 0.0 all-reduce.2.cloned.1.call-start
  8.0 64.5 %all-gather.4.cloned.1.call-done = f32[6144,128]{1,0:T(8,128)} async-done(((f32[192,128]{1,0:T(8,128)}), f32[6144,128]{1,0:T(8,128)}) %all-gather.4.cloned.1.call-update) | async-done | bytes 3145744 | tf_op jit(solution)/shard_map/all_gather | solution.py:17
  72.4 3.9 %fusion.5 = f32[64,128]{1,0:T(8,128)S(1)} fusion(f32[64,6144]{1,0:T(8,128)S(1)} %copy-done, f32[6144,128]{1,0:T(8,128)} %all-gather.4.cloned.1.call-done), kind=kOutput, calls=%fused_computation.14 | convolution fusion | flops 603979776 | bytes 4751360 | tf_op jit(solution)/shard_map/dot_general | solution.py:15
  76.3 0.9 fusion.6
  77.3 0.0 reduce-scatter.4.cloned.1.call-start
  77.3 4.4 %convolution_bitcast_fusion = f32[6144,128]{0,1:T(8,128)} fusion(f32[64,128]{1,0:T(8,128)S(1)} %fusion.5, f32[64,6144]{1,0:T(8,128)S(1)} %copy-done), kind=kOutput, calls=%fused_computation | convolution fusion | flops 603979776 | bytes 4751360 | tf_op jit(solution)/shard_map/dot_general | solution.py:26
  81.7 3.6 copy.10
  85.3 0.2 all-gather.6.cloned.1.call-start
  85.5 112.7 %all-reduce.2.cloned.1.call-done = f32[128,128]{0,1:T(8,128)} async-done(((f32[128,128]{0,1:T(8,128)}), f32[128,128]{0,1:T(8,128)}) %all-reduce.2.cloned.1.call-update) | async-done | bytes 65552 | tf_op jit(solution)/shard_map/psum | solution.py:37
  198.2 0.9 copy.8
  199.1 0.9 fusion.4
  200.0 11.7 %cholesky.16 = f32[128,128]{1,0:T(8,128)S(1)} custom-call(f32[128,128]{1,0:T(8,128)S(1)} %fusion.4), custom_call_target="Cholesky" | custom-call | tf_op jit(solution)/shard_map/jit(cholesky)/cholesky | solution.py:38
  211.7 0.6 compare_reduce_fusion
  212.4 0.7 fusion
  213.0 9.8 %custom-call.10 = f32[1,128,128]{1,2,0:T(8,128)S(1)} custom-call(f32[1,128,128]{2,1,0:T(8,128)S(1)} %fusion), custom_call_target="InvertDiagBlocksLowerTriangular" | custom-call | tf_op jit(solution)/shard_map/jit(_solve_triangular)/triangular_solve | solution.py:39
  222.9 80.8 %reduce-scatter.4.cloned.1.call-done = f32[192,128]{1,0:T(8,128)} async-done(((f32[6144,128]{1,0:T(8,128)}), f32[192,128]{1,0:T(8,128)}) %reduce-scatter.4.cloned.1.call-update) | async-done | bytes 98320
  303.6 1.1 fusion.1
  304.8 1.1 fusion.7
  305.9 0.8 convolution_multiply_fusion
  306.7 57.6 %all-gather.6.cloned.1.call-done = f32[4096,128]{1,0:T(8,128)} async-done(((f32[128,128]{1,0:T(8,128)}), f32[4096,128]{1,0:T(8,128)}) %all-gather.6.cloned.1.call-update) | async-done | bytes 2097168 | tf_op jit(solution)/shard_map/all_gather | solution.py:45
  364.2 1.7 reduce_sum.9
  365.9 0.6 broadcast_multiply_fusion
  (8 shorter events, 0.1 us)
Async XLA Ops:
  7.2 65.3 %copy-start = (f32[64,6144]{1,0:T(8,128)S(1)}, f32[64,6144]{1,0:T(8,128)}, u32[]{:S(2)}) copy-start(f32[64,6144]{1,0:T(8,128)} %param.2) | copy-start | bytes 4718596
  7.2 65.2 %all-gather.4.cloned.1.call-start = ((), (), s32[]{:S(2)}) async-start(), calls=%async_computation.1 | async-start | bytes 3244032 | tf_op jit(solution)/shard_map/all_gather | solution.py:17
  7.9 190.3 %all-reduce.2.cloned.1.call-start = ((), (), s32[]{:S(2)}) async-start(), calls=%async_computation.2 | async-start | bytes 131072 | tf_op jit(solution)/shard_map/psum | solution.py:37
  77.3 226.4 %reduce-scatter.4.cloned.1.call-start = ((), (), s32[]{:S(2)}) async-start(), calls=%async_computation.4 | async-start | bytes 3244032
  85.3 279.0 %all-gather.6.cloned.1.call-start = ((), (), s32[]{:S(2)}) async-start(), calls=%async_computation.3 | async-start | bytes 2162688 | tf_op jit(solution)/shard_map/all_gather | solution.py:45
  304.8 61.8 %copy-start.1 = (f32[128,192]{0,1:T(8,128)}, f32[128,192]{0,1:T(8,128)S(1)}, u32[]{:S(2)}) copy-start(f32[128,192]{0,1:T(8,128)S(1)} %fusion.1) | copy-start | bytes 294916
Sparse Core Ops, SparseCore 0:
  10.9 61.5 all-gather.3
  78.6 119.5 all-reduce.1
  203.6 99.9 reduce-scatter.3
  306.9 57.2 all-gather.5
